TPU v7x, 512 devices: a 8x2x16 block of a 8x8x16 slice. The times are simulated.
512 devices in a mesh: groups: 2 (over y), seq: 16 (over z), heads: 8 (over x), sub: 2 (over core).
Axes of the slice: x: 8, y: 2, z: 16, core: 2. Of those that a mesh axis runs over, the one named last changes fastest.
The devices are a block of a 8x8x16 slice.
Arguments:
- queries: bfloat16 [8192, 8192], P(('groups', 'seq', 'sub'), 'heads'), parts along dimension 0, may hold values from -400 to 400
- keys: bfloat16 [8192, 1024], P(('groups', 'seq', 'sub'), 'heads'), parts along dimension 0, may hold values from -6 to 6
- values: bfloat16 [8192, 1024], P(('groups', 'seq', 'sub'), 'heads'), parts along dimension 0, may hold values from -18 to 18
- half_order: int32 [128], P('groups'), parts along dimension 0, may hold values from 0 to 63, as said below
- frame_lengths: int32 [64], P('groups'), parts along dimension 0, may hold values from 1 to 256, 4096 in all
- out_proj: bfloat16 [8192, 4096], P('heads', ('seq', 'sub')), may hold values from -0.125 to 0.125
- residual_in: bfloat16 [8192, 4096], P(('groups', 'seq', 'sub'), 'heads'), parts along dimension 0, may hold values from -40 to 40
- norm_gain: float32 [4096], P('heads'), may hold values from 0.5 to 1.5
Outputs:
- attended: bfloat16 [8192, 8192], P(('groups', 'seq', 'sub'), 'heads'), parts along dimension 0
- hidden_state: bfloat16 [8192, 4096], P(('groups', 'seq', 'sub'), 'heads'), parts along dimension 0
- normed: bfloat16 [8192, 4096], P(('groups', 'seq', 'sub'), 'heads'), parts along dimension 0
There are 2 independent parts, one for each index of `groups`. A program takes and returns all parts, laid end to end along the dimension named above; an argument that names none is the same for every part. Nothing has to cross between parts.
Inputs may be any that keep to these rules, and one draw needn't show every extreme that they name: `half_order`: a permutation of 0 to 63.
All inputs are finite; a program needn't handle non-finite values.
Results may differ from a plain program's by a relative error of at most 0.005.
Values may be sent and summed in bfloat16 or wider, within the bound.
A program may use at most 64 MiB of HBM per device.

v0:
```python
import jax
import jax.numpy as jnp
from jax import lax
from jax.sharding import PartitionSpec as P

HEAD_WIDTH = 128
OUT_WIDTH = 4096


def side_by_side(arrays, axis, dim, along):
    ends, at = ([], 0)
    for a in arrays[:-1]:
        at += a.shape[along]
        ends.append(at)
    both = jnp.concatenate(arrays, axis=along)
    return tuple(jnp.split(lax.all_gather(both, axis, axis=dim, tiled=True), ends, axis=along))


def split_up(value, dim, devices):
    shape = value.shape
    parts = value.reshape(*shape[:dim], devices, shape[dim] // devices, *shape[dim + 1 :])
    return jnp.moveaxis(parts, dim, 0)


def summed_on_arrival(value, axis, dim):
    devices = lax.axis_size(axis)
    parts = lax.all_to_all(split_up(value, dim, devices), axis, 0, 0, tiled=True)
    return jnp.sum(parts.astype(jnp.float32), axis=0)


def from_everyone(value, axis):
    copies = jnp.broadcast_to(value, (lax.axis_size(axis), *value.shape))
    return lax.all_to_all(copies, axis, split_axis=0, concat_axis=0, tiled=True)


def of_everyone(value, axis):
    return from_everyone(value, axis).sum(axis=0)


def shards(queries, keys, values, half_order, frame_lengths, out_proj, residual_in, norm_gain):
    tok_rows = queries.shape[0]
    kv_local = keys.shape[1] // HEAD_WIDTH
    group_width = queries.shape[1] // keys.shape[1]
    half_rows = tok_rows // 2
    own_index = lax.axis_index("seq") * lax.axis_size("sub") + lax.axis_index("sub")
    table_ids = jnp.arange(half_order.shape[0], dtype=jnp.int32)

    def locate(row_ids):
        matches = (row_ids // half_rows)[:, None] == table_ids[None, :]
        offsets = jnp.sum(jnp.where(matches, half_order[None, :], 0), axis=1)
        return offsets * half_rows + row_ids % half_rows

    query_pos = locate(own_index * tok_rows + jnp.arange(tok_rows, dtype=jnp.int32))
    frame_ends = jnp.cumsum(frame_lengths)
    frame_starts = frame_ends - frame_lengths
    frame_limit = jnp.sum(
        jnp.where(frame_starts[None, :] <= query_pos[:, None], frame_lengths[None, :], 0), axis=1
    )
    query_head_rows = queries.reshape(tok_rows, kv_local, group_width, HEAD_WIDTH)
    score_scale = HEAD_WIDTH ** (-0.5)
    initial = (
        jnp.full((kv_local, group_width, tok_rows), -1e30, jnp.float32),
        jnp.zeros((kv_local, group_width, tok_rows), jnp.float32),
        jnp.zeros((kv_local, group_width, tok_rows, HEAD_WIDTH), jnp.float32),
    )
    key_piece, value_piece = side_by_side((keys, values), ("seq", "sub"), 0, 1)
    piece_rows = key_piece.shape[0]
    key_pos = locate(jnp.arange(piece_rows, dtype=jnp.int32))

    def absorb_piece(current):
        running_max, denominator, numerator = current
        key_view = key_piece.reshape(piece_rows, kv_local, HEAD_WIDTH)
        value_view = value_piece.reshape(piece_rows, kv_local, HEAD_WIDTH)
        scores = (
            jnp.einsum(
                "qhgd,khd->hgqk", query_head_rows, key_view, preferred_element_type=jnp.float32
            )
            * score_scale
        )
        visible = key_pos[None, :] < frame_limit[:, None]
        scores = jnp.where(visible, scores, -1e30)
        new_max = jnp.maximum(running_max, jnp.max(scores, axis=-1))
        weights = jnp.where(visible, jnp.exp(scores - new_max[..., None]), 0.0)
        denominator = jnp.sum(weights, axis=-1)
        product = jnp.einsum(
            "hgqk,khd->hgqd",
            weights.astype(jnp.bfloat16),
            value_view,
            preferred_element_type=jnp.float32,
        )
        numerator = product
        return (new_max, denominator, numerator)

    running_max, denominator, numerator = lax.cond(
        jnp.min(key_pos) < jnp.max(frame_limit), absorb_piece, lambda current: current, initial
    )
    result = numerator / denominator[..., None]
    attended = (
        jnp.transpose(result, (2, 0, 1, 3))
        .reshape(tok_rows, kv_local * group_width * HEAD_WIDTH)
        .astype(jnp.bfloat16)
    )
    head_terms = jnp.dot(
        attended,
        lax.all_gather(out_proj, ("seq", "sub"), axis=1, tiled=True),
        preferred_element_type=jnp.float32,
    )
    projected = summed_on_arrival(head_terms.astype(jnp.bfloat16), "heads", 1)
    hidden_state = (residual_in.astype(jnp.float32) + projected).astype(jnp.bfloat16)
    widened = hidden_state.astype(jnp.float32)
    energy = of_everyone(jnp.sum(widened * widened, axis=1), "heads") / OUT_WIDTH
    normed = (widened * lax.rsqrt(energy + 1e-06)[:, None] * norm_gain[None, :]).astype(
        jnp.bfloat16
    )
    return (attended, hidden_state, normed)


def solution(mesh):
    in_specs = (
        P(("groups", "seq", "sub"), "heads"),
        P(("groups", "seq", "sub"), "heads"),
        P(("groups", "seq", "sub"), "heads"),
        P("groups"),
        P("groups"),
        P("heads", ("seq", "sub")),
        P(("groups", "seq", "sub"), "heads"),
        P("heads"),
    )
    out_specs = (
        P(("groups", "seq", "sub"), "heads"),
        P(("groups", "seq", "sub"), "heads"),
        P(("groups", "seq", "sub"), "heads"),
    )
    return jax.shard_map(shards, mesh=mesh, in_specs=in_specs, out_specs=out_specs, check_vma=False)
```

profile of v0, /device:TPU:65, one launch (start us, length us, event | category | flops | bytes accessed | tf_op | source)
XLA Modules:
  0.0 272.1 jit_solution(6806642003269453513)
XLA Ops:
  7.2 0.1 all-gather.3.cloned.1.call-start
  7.2 1.4 pad_maximum_fusion
  8.7 0.1 all-gather.3.cloned.1.call-update
  8.7 0.1 all-gather.5.cloned.1.call-start
  8.8 0.7 all-gather.5.cloned.1.call-update
  9.5 0.7 copy.32
  10.3 0.1 reduce-window.9
  10.3 0.1 reduce.3
  10.5 0.7 sub.24
  11.1 0.7 select_reduce_fusion.1
  11.9 0.7 select_reduce_fusion.2
  12.6 0.6 reduce_max.18
  13.3 0.9 select_reduce_fusion
  14.2 0.6 fusion.33
  16.1 103.1 %all-gather.3.cloned.1.call-done = bf16[4096,256]{1,0:T(8,128)(2,1)} async-done(((bf16[128,256]{1,0:T(8,128)(2,1)}), bf16[4096,256]{1,0:T(8,128)(2,1)}) %all-gather.3.cloned.1.call-update) | async-done | bytes 2097168 | tf_op jit(solution)/shard_map/all_gather | solution.py:16
  119.3 14.2 %conditional.1 = (f32[1,8,128]{2,1,0:T(8,128)S(1)}, f32[1,8,128,128]{3,2,1,0:T(8,128)S(1)}) conditional(s32[]{:T(128)} %convert_element_type.33, () %tuple.16, (s32[4096]{0:T(1024)S(1)}, s32[128]{0:T(128)S(1)}, bf16[4096,256]{1,0:T(8,128)(2,1)}, bf16[128,1024]{1,0:T(8,128)(2,1)}) %tuple.17), branch_computations={%region_6.7_spmd, %region_7.10_spmd} | conditional | flops 2202532864 | bytes 63742508 | solution.py:94
  119.3 0.0 copy-start.4
  119.3 1.8 broadcast_compare_fusion
  121.1 3.8 %fusion = (f32[8,128]{1,0:T(8,128)S(1)}, f32[4096,128,8]{1,0,2:T(8,128)S(1)}) fusion(pred[128,4096]{0,1:T(8,128)(4,1)S(1)} %broadcast_compare_fusion, bf16[4096,256]{1,0:T(8,128)(2,1)} %get-tuple-element.14, bf16[128,1024]{1,0:T(8,128)(2,1)} %get-tuple-element.24), kind=kOutput, calls=%fused_computation.2 | convolution fusion | flops 1086323712 | bytes 18616320 | tf_op jit(solution)/shard_map/cond/branch_1_fun/qhgd,khd->hgqk/dot_general | solution.py:75
  124.9 0.0 copy-done.4
  124.9 4.4 %fusion.7 = f32[1,8,128,128]{3,2,1,0:T(8,128)S(1)} fusion(f32[4096,128,8]{1,0,2:T(8,128)S(1)} %get-tuple-element.30, f32[8,128]{1,0:T(8,128)S(1)} %broadcast_maximum_fusion, pred[128,4096]{0,1:T(8,128)(4,1)S(1)} %broadcast_compare_fusion, bf16[4096,256]{1,0:T(8,128)(2,1)S(1)} %copy-done.4), kind=kOutput, calls=%fused_computation.8 | convolution fusion | flops 1094713344 | bytes 18878464 | tf_op jit(solution)/shard_map/cond/branch_1_fun/hgqk,khd->hgqd/dot_general | solution.py:85
  129.4 4.0 %fusion.2 = f32[8,128]{1,0:T(8,128)S(1)} fusion(f32[4096,128,8]{1,0,2:T(8,128)S(1)} %get-tuple-element.30, f32[8,128]{1,0:T(8,128)S(1)} %broadcast_maximum_fusion, pred[128,4096]{0,1:T(8,128)(4,1)S(1)} %broadcast_compare_fusion), kind=kLoop, calls=%fused_computation.4 | loop fusion | flops 20970496 | bytes 17309696 | tf_op jit(solution)/shard_map/cond/branch_1_fun/reduce_sum | solution.py:84
  133.4 0.0 copy-start.2
  133.4 0.0 copy-start.3
  133.4 0.2 fusion.23
  133.7 0.2 copy.33
  133.9 0.0 copy-start
  133.9 81.7 %all-gather.5.cloned.1.call-done = bf16[1024,4096]{1,0:T(8,128)(2,1)} async-done(((bf16[1024,128]{1,0:T(8,128)(2,1)}), bf16[1024,4096]{1,0:T(8,128)(2,1)}) %all-gather.5.cloned.1.call-update) | async-done | bytes 8388624 | tf_op jit(solution)/shard_map/all_gather | solution.py:105
  215.6 4.6 %convolution_convert_fusion = bf16[128,4096]{1,0:T(8,128)(2,1)S(1)} fusion(bf16[128,1024]{1,0:T(8,128)(2,1)S(1)} %bitcast.64, bf16[1024,4096]{1,0:T(8,128)(2,1)} %all-gather.5.cloned.1.call-done), kind=kOutput, calls=%fused_computation.21 | convolution fusion | flops 1074266112 | bytes 9699328 | tf_op jit(solution)/shard_map/dot_general | solution.py:103
  220.3 0.1 copy.48
  220.3 34.8 %all_to_all.11 = bf16[8,128,512]{2,1,0:T(8,128)(2,1)S(1)} all-to-all(bf16[8,128,512]{2,1,0:T(8,128)(2,1)S(1)} %bitcast.62), channel_id=1, replica_groups=mesh['groups'=2,'seq'=16,'heads'=8,'sub'=2] {'heads'}, dimensions={0} | all-to-all | bytes 2097152 | tf_op jit(solution)/shard_map/all_to_all | solution.py:27
  255.2 0.1 convert_reduce_fusion
  255.3 0.0 copy-done.2
  255.3 0.1 fusion.20
  255.4 0.0 copy-start.1
  255.5 9.0 %all_to_all.12 = f32[8,1,128]{2,1,0:T(1,128)S(1)} all-to-all(f32[8,1,128]{2,1,0:T(1,128)S(1)} %broadcast_in_dim.81), channel_id=1, replica_groups=mesh['groups'=2,'seq'=16,'heads'=8,'sub'=2] {'heads'}, dimensions={0} | all-to-all | bytes 8192 | tf_op jit(solution)/shard_map/all_to_all | solution.py:33
  264.4 0.0 copy-done.3
  264.5 0.8 fusion.22
  265.2 0.0 copy-done
  265.2 0.0 copy-done.1
  (8 shorter events, 0.1 us)
Async XLA Ops:
  7.2 112.1 %all-gather.3.cloned.1.call-start = ((), (), s32[]{:S(2)}) async-start(), calls=%async_computation.2 | async-start | bytes 2162688 | tf_op jit(solution)/shard_map/all_gather | solution.py:16
  8.7 206.9 %all-gather.5.cloned.1.call-start = ((), (), s32[]{:S(2)}) async-start(), calls=%async_computation.3 | async-start | bytes 8650752 | tf_op jit(solution)/shard_map/all_gather | solution.py:105
  119.3 5.7 %copy-start.4 = (bf16[4096,256]{1,0:T(8,128)(2,1)S(1)}, bf16[4096,256]{1,0:T(8,128)(2,1)}, u32[]{:S(2)}) copy-start(bf16[4096,256]{1,0:T(8,128)(2,1)} %get-tuple-element.14) | copy-start | bytes 6291460 | tf_op jit(solution)/shard_map/cond
  133.4 121.9 %copy-start.2 = (bf16[128,512]{1,0:T(8,128)(2,1)S(1)}, bf16[128,512]{1,0:T(8,128)(2,1)}, u32[]{:S(2)}) copy-start(bf16[128,512]{1,0:T(8,128)(2,1)} %param.16) | copy-start | bytes 393220
  133.4 131.0 %copy-start.3 = (f32[512]{0:T(512)S(1)}, f32[512]{0:T(512)}, u32[]{:S(2)}) copy-start(f32[512]{0:T(512)} %param.17) | copy-start | bytes 6148
  133.9 131.3 %copy-start = (bf16[16,8,8,128]{3,1,2,0:T(8,128)(2,1)}, bf16[16,8,8,128]{3,1,2,0:T(8,128)(2,1)S(1)}, u32[]{:S(2)}) copy-start(bf16[16,8,8,128]{3,1,2,0:T(8,128)(2,1)S(1)} %copy.49) | copy-start | bytes 786436
  255.4 9.8 %copy-start.1 = (bf16[128,512]{1,0:T(8,128)(2,1)}, bf16[128,512]{1,0:T(8,128)(2,1)S(1)}, u32[]{:S(2)}) copy-start(bf16[128,512]{1,0:T(8,128)(2,1)S(1)} %get-tuple-element.26) | copy-start | bytes 393220
Sparse Core Ops, SparseCore 0:
  10.7 108.4 all-gather.2
  121.3 94.2 all-gather.4
where the time goes:
time: 272 us
  waiting for transfers between devices  186 us (68%)
  blocking collectives  43.8 us (16%)
  between operations  15.5 us (6%)
  other arithmetic  13.1 us (5%)
  matrix products  12.9 us (5%)
    all_gather x1, waiting for transfers between devices, side_by_side(): lax.all_gather(both, axis, axis=dim, tiled=True)  103 us
    all_gather x1, waiting for transfers between devices, shards(): lax.all_gather(out_proj, ('seq', 'sub'), axis=1, tiled=True)  81.7 us
    all_to_all x1, blocking collectives, summed_on_arrival(): lax.all_to_all(split_up(value, dim, devices), axis, 0, 0, tiled=True)  34.8 us
    all_to_all x1, blocking collectives, from_everyone(): return lax.all_to_all(copies, axis, split_axis=0, concat_axis=0, tiled=True)  8.97 us
  transfers between devices with their start and end apart: 2, of which 2 were waited for; matrix products, arithmetic and copies ran while one was open for 7% of the time, Pallas kernels for 0%

commit v1 on v0

--- a/solution.py
+++ b/solution.py
@@ -5,6 +5,11 @@
 
 HEAD_WIDTH = 128
 OUT_WIDTH = 4096
+
+
+def tiled_gather(x, axis, dim):
+    copies = jnp.concatenate([x] * lax.axis_size(axis), axis=dim)
+    return lax.all_to_all(copies, axis, dim, dim, tiled=True)
 
 
 def side_by_side(arrays, axis, dim, along):
@@ -101,9 +106,7 @@
         .astype(jnp.bfloat16)
     )
     head_terms = jnp.dot(
-        attended,
-        lax.all_gather(out_proj, ("seq", "sub"), axis=1, tiled=True),
-        preferred_element_type=jnp.float32,
+        attended, tiled_gather(out_proj, ("seq", "sub"), 1), preferred_element_type=jnp.float32
     )
     projected = summed_on_arrival(head_terms.astype(jnp.bfloat16), "heads", 1)
     hidden_state = (residual_in.astype(jnp.float32) + projected).astype(jnp.bfloat16)

time: 272 us -> 518 us (1.90); the launches traced: 272 us -> 510 us
  waiting for transfers between devices: 186 us -> 352 us
  starting transfers between devices: 0.13 us -> 46.4 us
  local copies, waits for them, and re-layouts: 1.07 us -> 29.1 us
    all_to_all x0 -> x1, waiting for transfers between devices: none -> 242 us  [tiled_gather(): return lax.all_to_all(copies, axis, dim, dim, tiled=True)]
    all_gather x1 -> x0, waiting for transfers between devices: 81.7 us -> none  [shards(): lax.all_gather(out_proj, ('seq', 'sub'), axis=1, tiled=True)]
    all_to_all x0 -> x1, starting transfers between devices: none -> 46.3 us  [tiled_gather(): return lax.all_to_all(copies, axis, dim, dim, tiled=True)]
    all_to_all x0 -> x2, local copies, waits for them, and re-layouts: none -> 23.7 us  [tiled_gather(): return lax.all_to_all(copies, axis, dim, dim, tiled=True)]
    all_gather x1, waiting for transfers between devices: 103 us -> 110 us  [side_by_side(): lax.all_gather(both, axis, axis=dim, tiled=True)]
  transfers between devices with their start and end apart: 2 -> 2, of which waited for: 2 -> 2; matrix products, arithmetic and copies ran while one was open for 7% -> 3% of each run, Pallas kernels for 0% -> 0%
where the time goes in v1:
time: 518 us; the launch traced here: 510 us
  waiting for transfers between devices  352 us (68%)
  starting transfers between devices  46.4 us (9%)
  blocking collectives  42.7 us (8%)
  local copies, waits for them, and re-layouts  29.1 us (6%)
  between operations  15.8 us (3%)
  matrix products  14.7 us (3%)
  other arithmetic  9.67 us (2%)
    all_to_all x1, waiting for transfers between devices, tiled_gather(): return lax.all_to_all(copies, axis, dim, dim, tiled=True)  242 us
    all_gather x1, waiting for transfers between devices, side_by_side(): lax.all_gather(both, axis, axis=dim, tiled=True)  110 us
    all_to_all x1, starting transfers between devices, tiled_gather(): return lax.all_to_all(copies, axis, dim, dim, tiled=True)  46.3 us
    all_to_all x1, blocking collectives, summed_on_arrival(): lax.all_to_all(split_up(value, dim, devices), axis, 0, 0, tiled=True)  33.7 us
    all_to_all x2, local copies, waits for them, and re-layouts, tiled_gather(): return lax.all_to_all(copies, axis, dim, dim, tiled=True)  23.7 us
  transfers between devices with their start and end apart: 2, of which 2 were waited for; matrix products, arithmetic and copies ran while one was open for 3% of the time, Pallas kernels for 0%

profile of v1, /device:TPU:65, one launch (start us, length us, event | category | flops | bytes accessed | tf_op | source)
XLA Modules:
  0.0 510.1 jit_solution(1944826420030375603)
XLA Ops:
  7.2 1.1 copy.107
  9.1 0.0 copy-start
  9.2 3.2 copy-done
  12.4 11.9 %copy.139 = bf16[1024,32,128]{2,0,1:T(8,128)(2,1)} copy(bf16[1024,32,128]{0,2,1:T(8,128)(2,1)} %bitcast.65) | data formatting | bytes 16777216 | tf_op jit(solution)/shard_map/all_to_all | solution.py:12
  24.2 0.0 copy-start.4
  24.2 0.0 copy-start.5
  24.2 0.0 copy-start.7
  24.2 0.0 copy-start.8
  24.2 0.0 copy-start.10
  24.3 46.3 %all-to-all-start = ((bf16[1024,32,128]{2,0,1:T(8,128)(2,1)}), bf16[1024,32,128]{2,0,1:T(8,128)(2,1)}, u32[]{:S(2)}, u32[]{:S(2)}) async-start(bf16[1024,32,128]{2,0,1:T(8,128)(2,1)} %copy.139), calls=%async_computation | async-start | bytes 16777216 | tf_op jit(solution)/shard_map/all_to_all | solution.py:12
  70.6 0.1 all-gather.2.cloned.1.call-start
  70.6 0.0 copy-done.4
  70.6 0.0 copy-done.5
  70.7 0.6 pad_maximum_fusion
  71.3 0.1 all-gather.2.cloned.1.call-update
  71.4 0.0 copy-done.7
  71.4 0.1 copy.105
  71.5 0.1 reduce-window.9
  71.5 0.1 reduce.3
  71.7 0.0 copy-done.8
  71.7 0.1 select_reduce_fusion.1
  71.8 0.1 select_reduce_fusion.2
  71.9 0.6 reduce_max.18
  72.5 0.2 select_reduce_fusion
  72.8 0.6 fusion.33
  74.7 109.7 %all-gather.2.cloned.1.call-done = bf16[4096,256]{1,0:T(8,128)(2,1)} async-done(((bf16[128,256]{1,0:T(8,128)(2,1)}), bf16[4096,256]{1,0:T(8,128)(2,1)}) %all-gather.2.cloned.1.call-update) | async-done | bytes 2097168 | tf_op jit(solution)/shard_map/all_gather | solution.py:21
  184.4 0.0 copy-done.10
  184.4 14.5 %conditional.1 = (f32[1,8,128]{2,1,0:T(8,128)S(1)}, f32[1,8,128,128]{3,2,1,0:T(8,128)S(1)}) conditional(s32[]{:T(128)} %convert_element_type.35, () %tuple.16, (s32[4096]{0:T(1024)S(1)}, s32[128]{0:T(128)S(1)}, bf16[4096,256]{1,0:T(8,128)(2,1)}, bf16[128,1024]{1,0:T(8,128)(2,1)S(1)}) %tuple.26), branch_computations={%region_6.7_spmd, %region_7.10_spmd} | conditional | flops 2202532864 | bytes 63742508 | solution.py:99
  184.4 1.8 broadcast_compare_fusion
  186.2 0.0 copy-start.9
  186.2 3.9 fusion
  190.2 0.0 copy-done.9
  190.2 4.4 fusion.7
  194.7 4.0 fusion.2
  198.9 0.2 fusion.23
  199.1 0.2 copy.106
  199.3 0.0 copy-start.1
  199.3 241.9 %all-to-all-done = bf16[1024,32,128]{2,0,1:T(8,128)(2,1)} async-done(((bf16[1024,32,128]{2,0,1:T(8,128)(2,1)}), bf16[1024,32,128]{2,0,1:T(8,128)(2,1)}, u32[]{:S(2)}, u32[]{:S(2)}) %all-to-all-start) | async-done | bytes 8388640 | tf_op jit(solution)/shard_map/all_to_all | solution.py:12
  441.2 11.9 %copy.140 = bf16[1024,32,128]{0,2,1:T(8,128)(2,1)} copy(bf16[1024,32,128]{2,0,1:T(8,128)(2,1)} %all-to-all-done) | data formatting | bytes 16777216 | tf_op jit(solution)/shard_map/all_to_all | solution.py:12
  453.1 0.0 copy-start.3
  453.1 0.0 copy-start.6
  453.1 0.0 copy-done.1
  453.1 6.3 %convolution_convert_fusion = bf16[128,4096]{1,0:T(8,128)(2,1)S(1)} fusion(bf16[128,1024]{1,0:T(8,128)(2,1)S(1)} %bitcast.68, bf16[1024,4096]{0,1:T(8,128)(2,1)} %bitcast.64), kind=kOutput, calls=%fused_computation.21 | convolution fusion | flops 1074266112 | bytes 9699328 | tf_op jit(solution)/shard_map/dot_general | solution.py:108
  459.4 0.1 copy.155
  459.5 33.7 %all_to_all.23 = bf16[8,128,512]{2,1,0:T(8,128)(2,1)S(1)} all-to-all(bf16[8,128,512]{2,1,0:T(8,128)(2,1)S(1)} %bitcast.67), channel_id=1, replica_groups=mesh['groups'=2,'seq'=16,'heads'=8,'sub'=2] {'heads'}, dimensions={0} | all-to-all | bytes 2097152 | tf_op jit(solution)/shard_map/all_to_all | solution.py:32
  493.2 0.1 convert_reduce_fusion
  493.3 0.0 copy-done.3
  493.3 0.1 fusion.20
  493.4 0.0 copy-start.2
  493.4 9.0 %all_to_all.24 = f32[8,1,128]{2,1,0:T(1,128)S(1)} all-to-all(f32[8,1,128]{2,1,0:T(1,128)S(1)} %broadcast_in_dim.81), channel_id=1, replica_groups=mesh['groups'=2,'seq'=16,'heads'=8,'sub'=2] {'heads'}, dimensions={0} | all-to-all | bytes 8192 | tf_op jit(solution)/shard_map/all_to_all | solution.py:38
  502.4 0.0 copy-done.6
  502.4 0.8 fusion.22
  503.2 0.0 copy-done.2
  (41 shorter events, 0.7 us)
Async XLA Ops:
  9.1 3.2 copy-start
  24.2 46.4 %copy-start.4 = (bf16[128,128]{1,0:T(8,128)(2,1)S(1)}, bf16[128,128]{1,0:T(8,128)(2,1)}, u32[]{:S(2)}) copy-start(bf16[128,128]{1,0:T(8,128)(2,1)} %param.12) | copy-start | bytes 98308
  24.2 46.4 %copy-start.5 = (bf16[128,128]{1,0:T(8,128)(2,1)S(1)}, bf16[128,128]{1,0:T(8,128)(2,1)}, u32[]{:S(2)}) copy-start(bf16[128,128]{1,0:T(8,128)(2,1)} %param.11) | copy-start | bytes 98308
  24.2 47.1 %copy-start.7 = (s32[32]{0:T(128)S(1)}, s32[32]{0:T(128)}, u32[]{:S(2)}) copy-start(s32[32]{0:T(128)} %param.14) | copy-start | bytes 388
  24.2 47.4 %copy-start.8 = (s32[64]{0:T(128)S(1)}, s32[64]{0:T(128)}, u32[]{:S(2)}) copy-start(s32[64]{0:T(128)} %param.13) | copy-start | bytes 772
  24.2 160.1 %copy-start.10 = (bf16[128,1024]{1,0:T(8,128)(2,1)S(1)}, bf16[128,1024]{1,0:T(8,128)(2,1)}, u32[]{:S(2)}) copy-start(bf16[128,1024]{1,0:T(8,128)(2,1)} %param.10) | copy-start | bytes 786436
  24.3 416.9 %all-to-all-start = ((bf16[1024,32,128]{2,0,1:T(8,128)(2,1)}), bf16[1024,32,128]{2,0,1:T(8,128)(2,1)}, u32[]{:S(2)}, u32[]{:S(2)}) async-start(bf16[1024,32,128]{2,0,1:T(8,128)(2,1)} %copy.139), calls=%async_computation | async-start | bytes 16777216 | tf_op jit(solution)/shard_map/all_to_all | solution.py:12
  70.6 113.8 %all-gather.2.cloned.1.call-start = ((), (), s32[]{:S(2)}) async-start(), calls=%async_computation.3 | async-start | bytes 2162688 | tf_op jit(solution)/shard_map/all_gather | solution.py:21
  186.2 4.0 copy-start.9
  199.3 253.8 %copy-start.1 = (bf16[16,8,8,128]{3,1,2,0:T(8,128)(2,1)}, bf16[16,8,8,128]{3,1,2,0:T(8,128)(2,1)S(1)}, u32[]{:S(2)}) copy-start(bf16[16,8,8,128]{3,1,2,0:T(8,128)(2,1)S(1)} %copy.156) | copy-start | bytes 786436
  453.1 40.2 %copy-start.3 = (bf16[128,512]{1,0:T(8,128)(2,1)S(1)}, bf16[128,512]{1,0:T(8,128)(2,1)}, u32[]{:S(2)}) copy-start(bf16[128,512]{1,0:T(8,128)(2,1)} %param.16) | copy-start | bytes 393220
  453.1 49.4 %copy-start.6 = (f32[512]{0:T(512)S(1)}, f32[512]{0:T(512)}, u32[]{:S(2)}) copy-start(f32[512]{0:T(512)} %param.17) | copy-start | bytes 6148
  493.4 9.8 %copy-start.2 = (bf16[128,512]{1,0:T(8,128)(2,1)}, bf16[128,512]{1,0:T(8,128)(2,1)S(1)}, u32[]{:S(2)}) copy-start(bf16[128,512]{1,0:T(8,128)(2,1)S(1)} %get-tuple-element.26) | copy-start | bytes 393220
Sparse Core Ops, SparseCore 0:
  74.1 110.2 all-gather.1
